TPU v7x, 128 devices: a whole 4x4x4 slice. The times are simulated.
128 devices in a mesh: pts: 16 (over z_hi, x, core), wlk: 8 (over z_lo, y).
Axes of the slice: x: 4, y: 4, z: 4 (z_hi: 2, z_lo: 2; z = z_hi * 2 + z_lo), core: 2. Of those that a mesh axis runs over, the one named last changes fastest.
Arguments:
- green_half: bfloat16 [16, 400, 2400], P('wlk'), may hold values from -6 to 6
- collocation: bfloat16 [2400, 9600], P('wlk', 'pts'), may hold values from -0.125 to 0.125
- occupied: bfloat16 [9600, 400], P('pts'), may hold values from -0.0029296875 to 0.0029296875
- kernel: bfloat16 [9600, 9600], P('pts'), may hold values from 0 to 16, as said below
Outputs:
- potential: float32 [16, 9600], P('wlk', 'pts')
- coulomb_energy: float32 [16], P('wlk')
- exchange_energy: float32 [16], P('wlk')
Inputs may be any that keep to these rules, and one draw needn't show every extreme that they name: kernel is symmetric and positive definite: kernel[p, q] equals kernel[q, p].
All inputs are finite; a program needn't handle non-finite values.
Results may differ from a plain program's by a relative error of at most 0.008.
Values may be sent and summed in bfloat16 or wider, within the bound.
A program may use at most 192 MiB of HBM per device.

v0:
```python
import jax
import jax.numpy as jnp
from jax import lax
from jax.sharding import PartitionSpec as P


def joined_along(tiles, dim):
    tiles = jnp.moveaxis(tiles, 0, dim)
    shape = tiles.shape
    return tiles.reshape(*shape[:dim], shape[dim] * shape[dim + 1], *shape[dim + 2 :])


def from_everyone(array, axis):
    copies = jnp.broadcast_to(array, (lax.axis_size(axis), *array.shape))
    return lax.all_to_all(copies, axis, split_axis=0, concat_axis=0, tiled=True)


def collect(array, axis, dim):
    return joined_along(from_everyone(array, axis), dim)


def passed_along(block, axis, distance):
    devices = range(lax.axis_size(axis))
    route = [((i - distance) % len(devices), i) for i in devices]
    return lax.ppermute(block, axis, route)


def taken_together(array, axis):
    return from_everyone(array, axis).sum(axis=0)


def packed_total(arrays, axis):
    ends = [0]
    for a in arrays:
        ends.append(ends[-1] + a.size)
    subtotal = taken_together(jnp.concatenate([a.ravel() for a in arrays]), axis)
    return tuple((subtotal[b:e].reshape(a.shape) for a, b, e in zip(arrays, ends, ends[1:])))


def local(green_half, collocation, occupied, kernel):
    pts_rows = occupied.shape[0]
    theta = jnp.einsum(
        "mp,wim->pwi",
        lax.all_gather(collocation, "wlk", axis=0, tiled=True),
        green_half,
        preferred_element_type=jnp.float32,
    ).astype(jnp.bfloat16)
    density = jnp.einsum("pwi,pi->wp", theta, occupied, preferred_element_type=jnp.float32)
    density_b = density.astype(jnp.bfloat16)

    def block_terms(start, theta_far, occ_far):
        cross_near = jnp.einsum("awi,bi->wab", theta, occ_far, preferred_element_type=jnp.float32)
        cross_far = jnp.einsum(
            "ai,bwi->wab", occupied, theta_far, preferred_element_type=jnp.float32
        )
        kernel_part = lax.dynamic_slice_in_dim(kernel, start, occ_far.shape[0], 1).astype(
            jnp.float32
        )
        return jnp.sum(kernel_part[None] * cross_near * cross_far, axis=(1, 2))

    density_all = collect(density_b, "pts", 1)
    potential = jnp.einsum("wq,aq->wa", density_all, kernel, preferred_element_type=jnp.float32)
    devices = lax.axis_size("pts")
    position = lax.axis_index("pts")
    exchange_sum = block_terms(position * pts_rows, theta, occupied)
    travel = (theta, occupied)
    for stride in range(1, devices // 2 + 1):
        travel = passed_along((travel[0], travel[1]), "pts", 1)
        source = (position - stride) % devices
        weight = 1.0 if 2 * stride == devices else 2.0
        exchange_sum = exchange_sum + weight * block_terms(source * pts_rows, travel[0], travel[1])
    coulomb = 0.5 * jnp.sum(density * potential, axis=1)
    coulomb_energy, exchange_energy = packed_total((coulomb, -0.5 * exchange_sum), "pts")
    return (potential, coulomb_energy, exchange_energy)


def solution(mesh):
    placed = (P("wlk", None, None), P("wlk", "pts"), P("pts", None), P("pts", None))
    return jax.shard_map(
        local,
        mesh=mesh,
        in_specs=placed,
        out_specs=(P("wlk", "pts"), P("wlk"), P("wlk")),
        check_vma=False,
    )
```

profile of v0, /device:TPU:1, one launch (start us, length us, event | category | flops | bytes accessed | tf_op | source)
XLA Modules:
  0.0 260.4 jit_solution(2479827401569120764)
XLA Ops:
  10.6 6.3 %collective-permute-done = bf16[600,400]{0,1:T(8,128)(2,1)S(1)} collective-permute-done((bf16[600,400]{0,1:T(8,128)(2,1)}, bf16[600,400]{0,1:T(8,128)(2,1)S(1)}, u32[]{:S(2)}, u32[]{:S(2)}) %collective-permute-start) | collective-permute-done | bytes 480032 | tf_op jit(solution)/shard_map/ppermute | solution.py:25
  19.2 6.0 %collective-permute-done.2 = bf16[600,400]{0,1:T(8,128)(2,1)S(1)} collective-permute-done((bf16[600,400]{0,1:T(8,128)(2,1)S(1)}, bf16[600,400]{0,1:T(8,128)(2,1)S(1)}, u32[]{:S(2)}, u32[]{:S(2)}) %collective-permute-start.2) | collective-permute-done | bytes 480032 | tf_op jit(solution)/shard_map/ppermute | solution.py:25
  27.7 13.2 %collective-permute-done.4 = bf16[600,400]{0,1:T(8,128)(2,1)S(1)} collective-permute-done((bf16[600,400]{0,1:T(8,128)(2,1)S(1)}, bf16[600,400]{0,1:T(8,128)(2,1)S(1)}, u32[]{:S(2)}, u32[]{:S(2)}) %collective-permute-start.4) | collective-permute-done | bytes 480032 | tf_op jit(solution)/shard_map/ppermute | solution.py:25
  42.8 16.5 %collective-permute-done.6 = bf16[600,400]{0,1:T(8,128)(2,1)S(1)} collective-permute-done((bf16[600,400]{0,1:T(8,128)(2,1)S(1)}, bf16[600,400]{0,1:T(8,128)(2,1)S(1)}, u32[]{:S(2)}, u32[]{:S(2)}) %collective-permute-start.6) | collective-permute-done | bytes 480032 | tf_op jit(solution)/shard_map/ppermute | solution.py:25
  59.3 5.8 %all-gather.3.cloned.1.call-done = bf16[8,300,600]{2,1,0:T(8,128)(2,1)} async-done(((bf16[1,300,600]{2,1,0:T(8,128)(2,1)}), bf16[8,300,600]{2,1,0:T(8,128)(2,1)}) %all-gather.3.cloned.1.call-update) | async-done | bytes 2880016 | tf_op jit(solution)/shard_map/all_gather | solution.py:44
  65.1 4.7 %reshape.24 = bf16[2400,600]{1,0:T(8,128)(2,1)} reshape(bf16[8,300,600]{2,1,0:T(8,128)(2,1)} %all-gather.3.cloned.1.call-done) | data formatting | bytes 5760000
  69.8 6.4 %multiply_reduce_fusion = (f32[600,2]{0,1:T(2,128)S(1)}, bf16[600,2,400]{0,2,1:T(8,128)(2,1)S(1)}) fusion(f32[600,400]{0,1:T(8,128)S(1)} %convert.2, bf16[2,400,2400]{2,1,0:T(8,128)(2,1)} %param.4, bf16[2400,600]{1,0:T(8,128)(2,1)} %reshape.24), kind=kOutput, calls=%fused_computation.20 | convolution fusion | flops 2305918720 | bytes 8644800 | tf_op jit(solution)/shard_map/mp,wim->pwi/dot_general | solution.py:42
  76.4 16.9 %collective-permute-done.10 = bf16[600,400]{0,1:T(8,128)(2,1)} collective-permute-done((bf16[600,400]{0,1:T(8,128)(2,1)S(1)}, bf16[600,400]{0,1:T(8,128)(2,1)}, u32[]{:S(2)}, u32[]{:S(2)}) %collective-permute-start.10) | collective-permute-done | bytes 480032 | tf_op jit(solution)/shard_map/ppermute | solution.py:25
  95.8 10.8 %dynamic-slice_convert_fusion.7 = (f32[600,600]{1,0:T(8,128)}, f32[600,600]{1,0:T(8,128)}, f32[600,600]{1,0:T(8,128)}, f32[600,600]{1,0:T(8,128)}, f32[600,600]{...) fusion(bf16[600,9600]{1,0:T(8,128)(2,1)} %param.7, ...), kind=kLoop, calls=%fused_computation.29 | loop fusion | flops 3240000 | bytes 19440036 | tf_op jit(solution)/shard_map/convert_element_type | solution.py:56
  106.7 3.1 %copy.55 = f32[600,600]{0,1:T(8,128)} copy(f32[600,600]{1,0:T(8,128)} %get-tuple-element.9) | data formatting | bytes 2880000 | tf_op jit(solution)/shard_map/convert_element_type | solution.py:56
  110.4 20.4 %all-to-all-start = ((bf16[16,2,600]{2,1,0:T(2,128)(2,1)}), bf16[16,2,600]{2,1,0:T(2,128)(2,1)S(1)}, u32[]{:S(2)}, u32[]{:S(2)}) async-start(bf16[16,2,600]{2,1,0:T(2,128)(2,1)} %broadcast_in_dim.4), calls=%async_computation | async-start | bytes 81920 | tf_op jit(solution)/shard_map/all_to_all | solution.py:15
  130.8 2.8 %fusion.38 = f32[600,2,600]{2,0,1:T(8,128)} fusion(bf16[600,2,400]{0,2,1:T(8,128)(2,1)S(1)} %get-tuple-element.15, bf16[600,400]{0,1:T(8,128)(2,1)S(1)} %copy-done), kind=kOutput, calls=%fused_computation.55 | convolution fusion | flops 576000000 | bytes 4320000 | tf_op jit(solution)/shard_map/awi,bi->wab/dot_general | solution.py:52
  135.2 3.9 %fusion.18 = f32[600,2,600]{2,0,1:T(8,128)} fusion(bf16[600,2,400]{0,2,1:T(8,128)(2,1)S(1)} %get-tuple-element.15, bf16[600,400]{0,1:T(8,128)(2,1)} %collective-permute-done.10), kind=kOutput, calls=%fused_computation.35 | convolution fusion | flops 576000000 | bytes 4320000 | tf_op jit(solution)/shard_map/awi,bi->wab/dot_general | solution.py:52
  139.1 3.9 %fusion.16 = f32[600,2,600]{2,0,1:T(8,128)} fusion(bf16[600,2,400]{0,2,1:T(8,128)(2,1)S(1)} %get-tuple-element.15, bf16[600,400]{0,1:T(8,128)(2,1)} %collective-permute-done.12), kind=kOutput, calls=%fused_computation.33 | convolution fusion | flops 576000000 | bytes 4320000 | tf_op jit(solution)/shard_map/awi,bi->wab/dot_general | solution.py:52
  142.9 2.8 %fusion.20 = f32[600,2,600]{2,0,1:T(8,128)} fusion(bf16[600,2,400]{0,2,1:T(8,128)(2,1)S(1)} %get-tuple-element.15, bf16[600,400]{0,1:T(8,128)(2,1)S(1)} %copy-done.27), kind=kOutput, calls=%fused_computation.37 | convolution fusion | flops 576000000 | bytes 4320000 | tf_op jit(solution)/shard_map/awi,bi->wab/dot_general | solution.py:52
  155.0 2.8 %fusion.26 = f32[600,2,600]{2,0,1:T(8,128)} fusion(bf16[600,2,400]{0,2,1:T(8,128)(2,1)S(1)} %get-tuple-element.15, bf16[600,400]{0,1:T(8,128)(2,1)S(1)} %copy-done.21), kind=kOutput, calls=%fused_computation.43 | convolution fusion | flops 576000000 | bytes 4320000 | tf_op jit(solution)/shard_map/awi,bi->wab/dot_general | solution.py:52
  157.8 3.1 %collective-permute-done.7 = bf16[600,2,400]{0,2,1:T(8,128)(2,1)} collective-permute-done((bf16[600,2,400]{0,2,1:T(8,128)(2,1)S(1)}, bf16[600,2,400]{0,2,1:T(8,128)(2,1)}, u32[]{:S(2)}, u32[]{:S(2)}) %collective-permute-start.7) | collective-permute-done | bytes 960032 | tf_op jit(solution)/shard_map/ppermute | solution.py:25
  166.2 3.6 %copy.56 = f32[600,2,600]{0,2,1:T(8,128)} copy(f32[600,2,600]{2,0,1:T(8,128)} %fusion.38) | data formatting | bytes 5760000 | tf_op jit(solution)/shard_map/awi,bi->wab/dot_general | solution.py:52
  169.8 3.8 %fusion.8 = f32[2]{0:T(128)S(1)} fusion(f32[600,2,600]{2,0,1:T(8,128)} %fusion.38, f32[600,2,600]{0,2,1:T(8,128)} %copy.56, f32[600,600]{0,1:T(8,128)} %copy.55), kind=kLoop, calls=%fused_computation.17 | loop fusion | flops 2159998 | bytes 7200008 | tf_op jit(solution)/shard_map/reduce_sum | solution.py:59
  173.6 3.8 %fusion.14 = f32[600,2,600]{2,0,1:T(8,128)} fusion(bf16[600,2,400]{0,2,1:T(8,128)(2,1)S(1)} %get-tuple-element.15, bf16[600,400]{0,1:T(8,128)(2,1)} %collective-permute-done.14), kind=kOutput, calls=%fused_computation.31 | convolution fusion | flops 576000000 | bytes 4320000 | tf_op jit(solution)/shard_map/awi,bi->wab/dot_general | solution.py:52
  177.9 8.2 %fusion.40 = (f32[2]{0:T(128)S(1)}, f32[2,600]{1,0:T(2,128)}) fusion(f32[600,2]{0,1:T(2,128)S(1)} %get-tuple-element.14, bf16[2,9600]{1,0:T(2,128)(2,1)S(1)} %reshape.22, bf16[600,9600]{1,0:T(8,128)(2,1)} %param.7), kind=kOutput, calls=%fused_computation.59 | convolution fusion | flops 23042398 | bytes 11568008 | tf_op jit(solution)/shard_map/wq,aq->wa/dot_general | solution.py:62
  200.1 6.9 %collective-permute-done.13 = bf16[600,2,400]{0,2,1:T(8,128)(2,1)S(1)} collective-permute-done((bf16[600,2,400]{0,2,1:T(8,128)(2,1)S(1)}, bf16[600,2,400]{0,2,1:T(8,128)(2,1)S(1)}, u32[]{:S(2)}, u32[]{:S(2)}) %collective-permute-start.13) | collective-permute-done | bytes 960032 | tf_op jit(solution)/shard_map/ppermute | solution.py:25
  213.3 11.2 %collective-permute-done.15 = bf16[600,2,400]{0,2,1:T(8,128)(2,1)S(1)} collective-permute-done((bf16[600,2,400]{0,2,1:T(8,128)(2,1)S(1)}, bf16[600,2,400]{0,2,1:T(8,128)(2,1)S(1)}, u32[]{:S(2)}, u32[]{:S(2)}) %collective-permute-start.15) | collective-permute-done | bytes 960032 | tf_op jit(solution)/shard_map/ppermute | solution.py:25
  225.9 27.0 %all_to_all.11 = f32[16,1,4]{2,1,0:T(1,128)S(1)} all-to-all(f32[16,1,4]{2,1,0:T(1,128)S(1)} %broadcast_in_dim.5), channel_id=1, replica_groups=mesh['pts'=16,'wlk'=8] {'pts'}, dimensions={0} | all-to-all | bytes 512 | tf_op jit(solution)/shard_map/all_to_all | solution.py:15
  (105 shorter events, 52.5 us)
Async XLA Ops:
  7.2 57.9 %all-gather.3.cloned.1.call-start = ((), (), s32[]{:S(2)}) async-start(), calls=%async_computation.2 | async-start | bytes 3502080 | tf_op jit(solution)/shard_map/all_gather | solution.py:44
  7.9 9.0 %collective-permute-start = (bf16[600,400]{0,1:T(8,128)(2,1)}, bf16[600,400]{0,1:T(8,128)(2,1)S(1)}, u32[]{:S(2)}, u32[]{:S(2)}) collective-permute-start(bf16[600,400]{0,1:T(8,128)(2,1)} %param.6), channel_id=1, source_target_pairs={{120,0},{0,8},{8,16},{16,24},{24,32},{32,40},{40,48},{48,56},{56,6... | collective-permute-start | bytes 1440008 | tf_op jit(solution)/shard_map/ppermute | solution.py:25
  16.9 48.2 %copy-start.18 = (bf16[600,400]{0,1:T(8,128)(2,1)}, bf16[600,400]{0,1:T(8,128)(2,1)S(1)}, u32[]{:S(2)}) copy-start(bf16[600,400]{0,1:T(8,128)(2,1)S(1)} %collective-permute-done) | copy-start | bytes 1440004
  16.9 8.4 %collective-permute-start.2 = (bf16[600,400]{0,1:T(8,128)(2,1)S(1)}, bf16[600,400]{0,1:T(8,128)(2,1)S(1)}, u32[]{:S(2)}, u32[]{:S(2)}) collective-permute-start(bf16[600,400]{0,1:T(8,128)(2,1)S(1)} %collective-permute-done), channel_id=1, source_target_pairs={{120,0},{0,8},{8,16},{16,24},{24,32},{32,40},{40,48},{48,56},{56,6... | collective-permute-start | bytes 1440008 | tf_op jit(solution)/shard_map/ppermute | solution.py:25
  25.2 39.9 %copy-start.20 = (bf16[600,400]{0,1:T(8,128)(2,1)}, bf16[600,400]{0,1:T(8,128)(2,1)S(1)}, u32[]{:S(2)}) copy-start(bf16[600,400]{0,1:T(8,128)(2,1)S(1)} %collective-permute-done.2) | copy-start | bytes 1440004
  25.2 15.6 %collective-permute-start.4 = (bf16[600,400]{0,1:T(8,128)(2,1)S(1)}, bf16[600,400]{0,1:T(8,128)(2,1)S(1)}, u32[]{:S(2)}, u32[]{:S(2)}) collective-permute-start(bf16[600,400]{0,1:T(8,128)(2,1)S(1)} %collective-permute-done.2), channel_id=1, source_target_pairs={{120,0},{0,8},{8,16},{16,24},{24,32},{32,40},{40,48},{48,56},{56,6... | collective-permute-start | bytes 1440008 | tf_op jit(solution)/shard_map/ppermute | solution.py:25
  41.7 17.6 %collective-permute-start.6 = (bf16[600,400]{0,1:T(8,128)(2,1)S(1)}, bf16[600,400]{0,1:T(8,128)(2,1)S(1)}, u32[]{:S(2)}, u32[]{:S(2)}) collective-permute-start(bf16[600,400]{0,1:T(8,128)(2,1)S(1)} %collective-permute-done.4), channel_id=1, source_target_pairs={{120,0},{0,8},{8,16},{16,24},{24,32},{32,40},{40,48},{48,56},{56,6... | collective-permute-start | bytes 1440008 | tf_op jit(solution)/shard_map/ppermute | solution.py:25
  59.3 10.5 %copy-start.24 = (bf16[600,400]{0,1:T(8,128)(2,1)}, bf16[600,400]{0,1:T(8,128)(2,1)S(1)}, u32[]{:S(2)}) copy-start(bf16[600,400]{0,1:T(8,128)(2,1)S(1)} %collective-permute-done.6) | copy-start | bytes 1440004
  59.3 16.9 %collective-permute-start.8 = (bf16[600,400]{0,1:T(8,128)(2,1)S(1)}, bf16[600,400]{0,1:T(8,128)(2,1)S(1)}, u32[]{:S(2)}, u32[]{:S(2)}) collective-permute-start(bf16[600,400]{0,1:T(8,128)(2,1)S(1)} %collective-permute-done.6), channel_id=1, source_target_pairs={{120,0},{0,8},{8,16},{16,24},{24,32},{32,40},{40,48},{48,56},{56,6... | collective-permute-start | bytes 1440008 | tf_op jit(solution)/shard_map/ppermute | solution.py:25
  76.2 19.6 %collective-permute-start.1 = (bf16[600,2,400]{0,2,1:T(8,128)(2,1)S(1)}, bf16[600,2,400]{0,2,1:T(8,128)(2,1)}, u32[]{:S(2)}, u32[]{:S(2)}) collective-permute-start(bf16[600,2,400]{0,2,1:T(8,128)(2,1)S(1)} %get-tuple-element.15), channel_id=1, source_target_pairs={{120,0},{0,8},{8,16},{16,24},{24,32},{32,40},{40,48},{48,56},{56,6... | collective-permute-start | bytes 2880008 | tf_op jit(solution)/shard_map/ppermute | solution.py:25
  76.3 19.6 %copy-start.26 = (bf16[600,400]{0,1:T(8,128)(2,1)}, bf16[600,400]{0,1:T(8,128)(2,1)S(1)}, u32[]{:S(2)}) copy-start(bf16[600,400]{0,1:T(8,128)(2,1)S(1)} %collective-permute-done.8) | copy-start | bytes 1440004
  76.3 16.9 %collective-permute-start.10 = (bf16[600,400]{0,1:T(8,128)(2,1)S(1)}, bf16[600,400]{0,1:T(8,128)(2,1)}, u32[]{:S(2)}, u32[]{:S(2)}) collective-permute-start(bf16[600,400]{0,1:T(8,128)(2,1)S(1)} %collective-permute-done.8), channel_id=1, source_target_pairs={{120,0},{0,8},{8,16},{16,24},{24,32},{32,40},{40,48},{48,56},{56,6... | collective-permute-start | bytes 1440008 | tf_op jit(solution)/shard_map/ppermute | solution.py:25
  93.2 16.5 %collective-permute-start.12 = (bf16[600,400]{0,1:T(8,128)(2,1)}, bf16[600,400]{0,1:T(8,128)(2,1)}, u32[]{:S(2)}, u32[]{:S(2)}) collective-permute-start(bf16[600,400]{0,1:T(8,128)(2,1)} %collective-permute-done.10), channel_id=1, source_target_pairs={{120,0},{0,8},{8,16},{16,24},{24,32},{32,40},{40,48},{48,56},{56,6... | collective-permute-start | bytes 1440008 | tf_op jit(solution)/shard_map/ppermute | solution.py:25
  95.8 37.8 %collective-permute-start.3 = (bf16[600,2,400]{0,2,1:T(8,128)(2,1)}, bf16[600,2,400]{0,2,1:T(8,128)(2,1)}, u32[]{:S(2)}, u32[]{:S(2)}) collective-permute-start(bf16[600,2,400]{0,2,1:T(8,128)(2,1)} %collective-permute-done.1), channel_id=1, source_target_pairs={{120,0},{0,8},{8,16},{16,24},{24,32},{32,40},{40,48},{48,56},{56,6... | collective-permute-start | bytes 2880008 | tf_op jit(solution)/shard_map/ppermute | solution.py:25
  106.7 24.1 %copy-start = (bf16[600,400]{0,1:T(8,128)(2,1)S(1)}, bf16[600,400]{0,1:T(8,128)(2,1)}, u32[]{:S(2)}) copy-start(bf16[600,400]{0,1:T(8,128)(2,1)} %param.6) | copy-start | bytes 1440004
  109.7 63.9 %collective-permute-start.14 = (bf16[600,400]{0,1:T(8,128)(2,1)}, bf16[600,400]{0,1:T(8,128)(2,1)}, u32[]{:S(2)}, u32[]{:S(2)}) collective-permute-start(bf16[600,400]{0,1:T(8,128)(2,1)} %collective-permute-done.12), channel_id=1, source_target_pairs={{120,0},{0,8},{8,16},{16,24},{24,32},{32,40},{40,48},{48,56},{56,6... | collective-permute-start | bytes 1440008 | tf_op jit(solution)/shard_map/ppermute | solution.py:25
  110.4 67.1 %all-to-all-start = ((bf16[16,2,600]{2,1,0:T(2,128)(2,1)}), bf16[16,2,600]{2,1,0:T(2,128)(2,1)S(1)}, u32[]{:S(2)}, u32[]{:S(2)}) async-start(bf16[16,2,600]{2,1,0:T(2,128)(2,1)} %broadcast_in_dim.4), calls=%async_computation | async-start | bytes 81920 | tf_op jit(solution)/shard_map/all_to_all | solution.py:15
  133.6 13.4 %collective-permute-start.5 = (bf16[600,2,400]{0,2,1:T(8,128)(2,1)}, bf16[600,2,400]{0,2,1:T(8,128)(2,1)S(1)}, u32[]{:S(2)}, u32[]{:S(2)}) collective-permute-start(bf16[600,2,400]{0,2,1:T(8,128)(2,1)} %collective-permute-done.3), channel_id=1, source_target_pairs={{120,0},{0,8},{8,16},{16,24},{24,32},{32,40},{40,48},{48,56},{56,6... | collective-permute-start | bytes 2880008 | tf_op jit(solution)/shard_map/ppermute | solution.py:25
  147.0 13.9 %collective-permute-start.7 = (bf16[600,2,400]{0,2,1:T(8,128)(2,1)S(1)}, bf16[600,2,400]{0,2,1:T(8,128)(2,1)}, u32[]{:S(2)}, u32[]{:S(2)}) collective-permute-start(bf16[600,2,400]{0,2,1:T(8,128)(2,1)S(1)} %collective-permute-done.5), channel_id=1, source_target_pairs={{120,0},{0,8},{8,16},{16,24},{24,32},{32,40},{40,48},{48,56},{56,6... | collective-permute-start | bytes 2880008 | tf_op jit(solution)/shard_map/ppermute | solution.py:25
  160.9 16.8 %collective-permute-start.9 = (bf16[600,2,400]{0,2,1:T(8,128)(2,1)}, bf16[600,2,400]{0,2,1:T(8,128)(2,1)}, u32[]{:S(2)}, u32[]{:S(2)}) collective-permute-start(bf16[600,2,400]{0,2,1:T(8,128)(2,1)} %collective-permute-done.7), channel_id=1, source_target_pairs={{120,0},{0,8},{8,16},{16,24},{24,32},{32,40},{40,48},{48,56},{56,6... | collective-permute-start | bytes 2880008 | tf_op jit(solution)/shard_map/ppermute | solution.py:25
  177.6 12.1 %collective-permute-start.11 = (bf16[600,2,400]{0,2,1:T(8,128)(2,1)}, bf16[600,2,400]{0,2,1:T(8,128)(2,1)S(1)}, u32[]{:S(2)}, u32[]{:S(2)}) collective-permute-start(bf16[600,2,400]{0,2,1:T(8,128)(2,1)} %collective-permute-done.9), channel_id=1, source_target_pairs={{120,0},{0,8},{8,16},{16,24},{24,32},{32,40},{40,48},{48,56},{56,6... | collective-permute-start | bytes 2880008 | tf_op jit(solution)/shard_map/ppermute | solution.py:25
  189.7 17.2 %collective-permute-start.13 = (bf16[600,2,400]{0,2,1:T(8,128)(2,1)S(1)}, bf16[600,2,400]{0,2,1:T(8,128)(2,1)S(1)}, u32[]{:S(2)}, u32[]{:S(2)}) collective-permute-start(bf16[600,2,400]{0,2,1:T(8,128)(2,1)S(1)} %collective-permute-done.11), channel_id=1, source_target_pairs={{120,0},{0,8},{8,16},{16,24},{24,32},{32,40},{40,48},{48,56},{56,6... | collective-permute-start | bytes 2880008 | tf_op jit(solution)/shard_map/ppermute | solution.py:25
  207.0 17.6 %collective-permute-start.15 = (bf16[600,2,400]{0,2,1:T(8,128)(2,1)S(1)}, bf16[600,2,400]{0,2,1:T(8,128)(2,1)S(1)}, u32[]{:S(2)}, u32[]{:S(2)}) collective-permute-start(bf16[600,2,400]{0,2,1:T(8,128)(2,1)S(1)} %collective-permute-done.13), channel_id=1, source_target_pairs={{120,0},{0,8},{8,16},{16,24},{24,32},{32,40},{40,48},{48,56},{56,6... | collective-permute-start | bytes 2880008 | tf_op jit(solution)/shard_map/ppermute | solution.py:25
  212.0 12.6 %copy-start.4 = (f32[600,2,600]{2,0,1:T(8,128)S(1)}, f32[600,2,600]{2,0,1:T(8,128)}, u32[]{:S(2)}) copy-start(f32[600,2,600]{2,0,1:T(8,128)} %fusion.14) | copy-start | bytes 8640004
  (22 other events, 107.1 us)
Sparse Core Ops, SparseCore 0:
  9.6 55.4 all-gather.2
where the time goes:
time: 261 us; the launch traced here: 260 us
  waiting for transfers between devices  88.6 us (34%)
  matrix products  58.9 us (23%)
  starting transfers between devices  40 us (15%)
  blocking collectives  27 us (10%)
  local copies, waits for them, and re-layouts  15.9 us (6%)
  other arithmetic  15.8 us (6%)
  between operations  14.2 us (5%)
    ppermute x16, waiting for transfers between devices, passed_along(): return lax.ppermute(block, axis, route)  82.1 us
    dot_general x9, matrix products, block_terms(): jnp.einsum('awi,bi->wab', theta, occ_far, preferred_element_type=jnp.floa...  28.3 us
    all_to_all x1, blocking collectives, from_everyone(): return lax.all_to_all(copies, axis, split_axis=0, concat_axis=0, tiled=True)  27 us
    all_to_all x1, starting transfers between devices, from_everyone(): return lax.all_to_all(copies, axis, split_axis=0, concat_axis=0, tiled=True)  20.4 us
    ppermute x16, starting transfers between devices, passed_along(): return lax.ppermute(block, axis, route)  19.6 us
    dot_general x8, matrix products, block_terms(): jnp.einsum('ai,bwi->wab', occupied, theta_far, preferred_element_type=jnp...  16 us
    convert_element_type x1, other arithmetic, block_terms(): lax.dynamic_slice_in_dim(kernel, start, occ_far.shape[0], 1)  10.8 us
    dot_general x1, matrix products, local(): jnp.einsum('wq,aq->wa', density_all, kernel, preferred_element_type=jnp.f...  8.23 us
  transfers between devices with their start and end apart: 18, of which 11 were waited for; matrix products, arithmetic and copies ran while one was open for 33% of the time, Pallas kernels for 0%

commit v1 on v0

v1 whole, which is shorter than its diff:
```python
import jax
import jax.numpy as jnp
from jax import lax
from jax.experimental import pallas as pl
from jax.experimental.pallas import tpu as pltpu
from jax.sharding import PartitionSpec as P

MESH = pl.DeviceIdType.MESH
F32, BF16 = jnp.float32, jnp.bfloat16

ELEC = 400
PTS = 600
PAD = 640
ROWS = 608
DEEP = 300
DEEP_PAD = 304
GROUPS = 8
C_CUT = 160
KCH = 160
CHUNK = ((0, 384), (384, 256))
STEPS = ((0, 3), (3, 5))
FLOWS = 96


def dot(a, b):
    return jnp.dot(a, b, preferred_element_type=F32)


def body(green, colloc, occ, kmat, pot_out, sum_out,
         cin, oin, gv, g8, kst, kb, cbuf, acc, ttown, ttbuf, tp, op, otown, otbuf,
         trans, dens, dbuf, ebuf, exch, pot, local_sem, send, recv, d_send, d_recv, e_send, e_recv):
    a, g = lax.axis_index("pts"), lax.axis_index("wlk")
    zh, x, c = a // 8, (a // 2) % 4, a % 2
    zl, y = g // 4, g % 4
    z = zh * 2 + zl
    is_same = zh == zl
    is_cross = zh != zl
    same = is_same.astype(jnp.int32)

    def at(zz, xx, cc, yy):
        return {"pts": (zz // 2) * 8 + xx * 2 + cc, "wlk": (zz % 2) * 4 + yy}

    sib = at(z, x, 1 - c, y)
    right, left = at(z, (x + 1) % 4, c, y), at(z, (x + 3) % 4, c, y)
    up, down = at(z, x, c, (y + 1) % 4), at(z, x, c, (y + 3) % 4)
    zmate = at(zh * 2 + 1 - zl, x, c, y)
    xmate = at(3 - z, x, c, y)
    lanes = tuple(pl.ds(pl.multiple_of(2 * start + c * size, 128), size) for start, size in CHUNK)
    cols = tuple(pl.ds(start, size) for start, size in CHUNK)
    numbers = iter(range(FLOWS))

    def flow(src, dst, dev):
        f = next(numbers)
        return pltpu.make_async_remote_copy(
            src_ref=src, dst_ref=dst, send_sem=send.at[f], recv_sem=recv.at[f],
            device_id=dev, device_id_type=MESH)

    def start(*copies):
        for cp in copies:
            cp.start()

    load_c = pltpu.make_async_copy(colloc, cin, local_sem.at[0])
    load_o = pltpu.make_async_copy(occ, oin, local_sem.at[1])
    load_g = [pltpu.make_async_copy(green.at[w], gv.at[pl.ds(w * ELEC, ELEC)], local_sem.at[2 + w]) for w in range(2)]
    pieces = [(s, min(KCH, PTS - s)) for s in range(0, PTS, KCH)]
    load_k = [pltpu.make_async_copy(kmat.at[pl.ds(s, n)], kst.at[i % 2, pl.ds(0, n)], local_sem.at[4 + i])
              for i, (s, n) in enumerate(pieces)]
    start(load_c, load_o)

    plane = z * 8 + x * 2 + c

    def plane_dev(r):
        q = (plane + r) % 32
        return at(q // 8, (q // 2) % 4, q % 2, y)

    barrier = pltpu.get_barrier_semaphore()
    for dev in (up, down):
        pl.semaphore_signal(barrier, inc=1, device_id=dev, device_id_type=MESH)

    def greet(r, carry):
        pl.semaphore_signal(barrier, inc=1, device_id=plane_dev(r), device_id_type=MESH)
        return carry

    lax.fori_loop(1, 32, greet, 0)
    cbuf[g, :, pl.ds(PAD - 128, 128)] = jnp.zeros((DEEP_PAD, 128), BF16)
    cbuf[g, pl.ds(DEEP_PAD - 16, 16), :] = jnp.zeros((16, PAD), BF16)
    load_c.wait()
    cbuf[g, pl.ds(0, DEEP), pl.ds(0, PTS)] = cin[...]
    start(*load_g)
    load_o.wait()
    otown[:, pl.ds(PAD - 128, 128)] = jnp.zeros((ELEC, 128), BF16)
    otown[:, pl.ds(0, PTS)] = oin[...]

    @pl.when(is_same)
    def _():
        for h in range(2):
            otbuf[0, :, lanes[h]] = otown[:, cols[h]]

    pl.semaphore_wait(barrier, 33)

    def slot(zlo, yy):
        return zlo * 4 + yy

    def c_flow(k, h, dev, first=0, count=DEEP_PAD):
        ref = cbuf.at[k, pl.ds(first, count), cols[h]]
        return flow(ref, ref, dev)

    own_k, mate_k = slot(zl, y), slot(1 - zl, y)
    dn, un, on = (y + 3) % 4, (y + 1) % 4, (y + 2) % 4
    c_z, c_own, c_mate, c_far, c_matefar = [], [], [], [], []
    for h in range(2):
        c_z.append(c_flow(own_k, h, zmate))
        c_own.append((c_flow(own_k, h, up), c_flow(own_k, h, down)))
        c_mate.append((c_flow(mate_k, h, up), c_flow(mate_k, h, down)))
        c_far.append((c_flow(slot(zl, dn), h, up, 0, C_CUT),
                      c_flow(slot(zl, un), h, down, C_CUT, DEEP_PAD - C_CUT)))
        c_matefar.append((c_flow(slot(1 - zl, dn), h, up, 0, C_CUT),
                          c_flow(slot(1 - zl, un), h, down, C_CUT, DEEP_PAD - C_CUT)))
    start(c_own[0][0], c_own[0][1], c_z[0], c_z[1])

    def o_block(i, h):
        return otbuf.at[i, :, lanes[h]]

    o_xx = [flow(otown.at[:, cols[h]], o_block(0, h), xmate) for h in range(2)]
    o_right = [flow(o_block(0, h), o_block(1, h), right) for h in range(2)]
    o_left = [flow(o_block(0, h), o_block(2, h), left) for h in range(2)]
    o_sib = [flow(o_block(0, h), o_block(0, h), sib) for h in range(2)]
    o_far = [flow(o_block(1, 0), o_block(3, 0), right), flow(o_block(2, 1), o_block(3, 1), left)]
    o_relay = [[flow(o_block(i, h), o_block(i, h), sib) for h in range(2)] for i in (1, 2, 3)]
    o_first = [o_right[0], o_left[0], o_right[1], o_left[1]] + o_sib

    @pl.when(is_cross)
    def _():
        start(*o_xx)

    @pl.when(is_same)
    def _():
        start(*o_first)

    for cp in load_g:
        cp.wait()
    start(load_k[0], load_k[1])

    def cut_green(r, carry):
        rows = pl.ds(pl.multiple_of(r * 80, 16), 80)
        piece = gv[rows, :]
        for k in range(GROUPS):
            part = piece[:, k * DEEP:(k + 1) * DEEP]
            g8[k, rows, pl.ds(0, DEEP_PAD)] = jnp.concatenate([part, jnp.zeros((80, DEEP_PAD - DEEP), BF16)], axis=1)
        return carry

    lax.fori_loop(0, 10, cut_green, 0)

    def add_theta(k, h, first=False):
        part = dot(g8[k, :, pl.ds(0, DEEP_PAD)], cbuf[k, :, cols[h]])
        if first:
            acc[:, cols[h]] = part
        else:
            acc[:, cols[h]] += part

    def cut_kernel(i):
        s, n = pieces[i]
        load_k[i].wait()

        def rows_at(r, carry):
            rows = pl.ds(pl.multiple_of(r * 16, 16), 16)
            out = pl.ds(pl.multiple_of(s + r * 16, 16), 16)
            for b in range(16):
                j, core = b // 2, b % 2
                kb[j, out, pl.ds(core * 384, 384)] = kst[i % 2, rows, pl.ds(b * PTS, 384)]
                part = kst[i % 2, rows, pl.ds(b * PTS + 384, PTS - 384)]
                kb[j, out, pl.ds(768 + core * 256, 256)] = jnp.concatenate(
                    [part, jnp.zeros((16, PAD - PTS), BF16)], axis=1)
            return carry

        lax.fori_loop(0, (n + 15) // 16, rows_at, 0)
        if i + 2 < len(pieces):
            load_k[i + 2].start()

    add_theta(own_k, 0, True)
    add_theta(own_k, 1, True)

    c_z[0].wait_recv()
    start(*c_mate[0])
    c_own[0][0].wait_recv()
    c_far[0][0].start()
    c_own[0][1].wait_recv()
    c_far[0][1].start()
    start(*c_own[1])
    add_theta(mate_k, 0)
    add_theta(slot(zl, dn), 0)
    add_theta(slot(zl, un), 0)
    c_z[1].wait_recv()
    start(*c_mate[1])
    cut_kernel(0)
    c_mate[0][0].wait_recv()
    c_matefar[0][0].start()
    c_mate[0][1].wait_recv()
    c_matefar[0][1].start()
    add_theta(slot(1 - zl, dn), 0)
    add_theta(slot(1 - zl, un), 0)

    @pl.when(is_cross)
    def _():
        for cp in o_xx:
            cp.wait_recv()
        start(*o_first)

    add_theta(mate_k, 1)
    c_far[0][0].wait_recv()
    c_far[0][1].wait_recv()
    add_theta(slot(zl, on), 0)
    c_own[1][0].wait_recv()
    c_far[1][0].start()
    c_own[1][1].wait_recv()
    c_far[1][1].start()
    add_theta(slot(zl, dn), 1)
    c_matefar[0][0].wait_recv()
    c_matefar[0][1].wait_recv()
    add_theta(slot(1 - zl, on), 0)

    def t_block(i, h):
        return ttbuf.at[i, :, lanes[h]]

    def t_flows(count, make):
        return [[make(w, h) for h in range(2)] for w in range(count)]

    t_z = t_flows(2, lambda w, h: flow(ttown.at[w, :, cols[h]], t_block(2 + w, h), zmate))
    t_xx = t_flows(2, lambda w, h: flow(ttown.at[w, :, cols[h]], t_block(w, h), xmate))
    t_sib = t_flows(2, lambda w, h: flow(t_block(w, h), t_block(w, h), sib))
    t_sibz = t_flows(2, lambda w, h: flow(t_block(2 + w, h), t_block(2 + w, h), sib))
    t_right = t_flows(2, lambda w, h: flow(t_block(w * (1 + same), h), t_block(4 + w, h), right))
    t_left = t_flows(2, lambda w, h: flow(t_block(same + w * (1 + same), h), t_block(6 + w, h), left))
    low_r = (x + 1) % 4 < 2
    low_l = (x + 3) % 4 < 2
    go_r = 4 + jnp.where(is_same & jnp.logical_not(low_r), 1, 0)
    go_l = 6 + jnp.where(is_same & low_l, 0, 1)
    t_far = [[flow(t_block(go_r, h), t_block(8, h), right) for h in range(2)],
             [flow(t_block(go_l, h), t_block(9, h), left) for h in range(2)]]
    t_relay = [[flow(t_block(i, h), t_block(i, h), sib) for h in range(2)] for i in range(4, 10)]

    def publish(h):
        for w in range(2):
            t = acc[pl.ds(w * ELEC, ELEC), cols[h]].astype(BF16)
            ttown[w, :, cols[h]] = t

            @pl.when(is_same)
            def _():
                ttbuf[w, :, lanes[h]] = t

            dens[pl.ds(w, 1), cols[h]] = jnp.sum(
                t.astype(F32) * otown[:, cols[h]].astype(F32), axis=0, keepdims=True)

        @pl.when(is_cross)
        def _():
            start(t_xx[0][h], t_z[0][h], t_xx[1][h], t_z[1][h])

        @pl.when(is_same)
        def _():
            start(t_z[0][h], t_right[0][h], t_left[0][h], t_z[1][h], t_sib[0][h], t_sib[1][h])

    publish(0)

    c_mate[1][0].wait_recv()
    c_matefar[1][0].start()
    c_mate[1][1].wait_recv()
    c_matefar[1][1].start()
    add_theta(slot(zl, un), 1)
    add_theta(slot(1 - zl, dn), 1)
    add_theta(slot(1 - zl, un), 1)

    for h in range(2):
        o_right[h].wait_recv()
        o_left[h].wait_recv()
    start(*o_far, *o_relay[0], *o_relay[1])
    trans[...] = jnp.zeros_like(trans)

    c_far[1][0].wait_recv()
    c_far[1][1].wait_recv()
    add_theta(slot(zl, on), 1)
    c_matefar[1][0].wait_recv()
    c_matefar[1][1].wait_recv()
    add_theta(slot(1 - zl, on), 1)
    publish(1)

    dbuf[a] = dens[...].astype(BF16).astype(F32)

    def d_flow(r):
        return pltpu.make_async_remote_copy(
            src_ref=dbuf.at[a], dst_ref=dbuf.at[a], send_sem=d_send.at[r], recv_sem=d_recv.at[r],
            device_id={"pts": (a + r) % 16, "wlk": g}, device_id_type=MESH)

    def d_start(r, carry):
        d_flow(r).start()
        return carry

    def d_wait(r, carry):
        d_flow(r).wait()
        return carry

    lax.fori_loop(1, 16, d_start, 0)

    def turned(src, size):
        trans[pl.ds(0, ELEC), pl.ds(0, size)] = src.astype(F32)
        return jnp.swapaxes(trans[:, pl.ds(0, size)], 0, 1).astype(BF16)

    def turn(side, h):
        tp[side, cols[h], :] = turned(ttbuf[side, :, lanes[h]], CHUNK[h][1])

    def potential():
        pot[...] = jnp.zeros_like(pot)

        def add_chip(j, carry):
            one, two = dbuf[2 * j].astype(BF16), dbuf[2 * j + 1].astype(BF16)
            both = jnp.concatenate([one[:, :384], two[:, :384], one[:, 384:], two[:, 384:]], axis=1)
            pot[...] += lax.dot_general(both, kb[j], (((1,), (1,)), ((), ())), preferred_element_type=F32)
            return carry

        lax.fori_loop(0, 8, add_chip, 0)
        pot_out[...] = pot[:, pl.ds(0, PTS)]

    exch[...] = jnp.zeros_like(exch)

    def unit(tt, side, ot, chip, weight, h):
        left_t = tp[side, pl.ds(0, ROWS), pl.ds(0, ELEC)]
        left_o = op[pl.ds(0, ROWS), pl.ds(0, ELEC)]

        def step(n, carry):
            part = pl.ds(pl.multiple_of(n * 256, 256), 256)
            near = dot(left_t, otbuf[ot, :, part])
            away = dot(left_o, ttbuf[tt, :, part])
            terms = kb[chip, :, part].astype(F32) * near * away
            return carry + terms.reshape(ROWS // 8, 8, 256).sum(axis=0)

        total = lax.fori_loop(*STEPS[h], step, jnp.zeros((8, 256), F32))
        exch[side] += weight * total

    far_zh = jnp.where(is_same, zh, 1 - zh) * 4
    chip_0, chip_1, chip_2, chip_3 = (far_zh + (x + d) % 4 for d in (0, 3, 1, 2))
    cross2 = 2 * (1 - same)
    self_weight = jnp.where(is_same, 1.0, 2.0)
    far_side = jnp.where(is_cross | (x >= 2), 2, 0)
    units = {
        0: (cross2, 0, chip_0, self_weight), 1: (cross2 + 1, 0, chip_0, self_weight),
        2: (2, 0, chip_0, self_weight), 3: (3, 0, chip_0, self_weight),
        4: (cross2, 1, chip_1, 2.0), 5: (3 - same, 1, chip_1, 2.0),
        6: (cross2 + same, 2, chip_2, 2.0), 7: (3, 2, chip_2, 2.0),
        8: (far_side, 3, chip_3, 2.0), 9: (far_side + 1, 3, chip_3, 2.0),
    }

    def run(tt, h):
        unit(tt, *units[tt], h)

    def pass_on(w, h):
        @pl.when(is_same)
        def _():
            t_z[w][h].wait_recv()
            start(t_right[1][h] if w == 0 else t_left[1][h], t_sibz[w][h])

        @pl.when(is_cross)
        def _():
            t_xx[w][h].wait_recv()
            start(t_right[w][h], t_left[w][h], t_sib[w][h])
            t_z[w][h].wait_recv()

        turn(2 + w, h)

    def arrive(first, second, h):
        t_right[first][h].wait_recv()
        t_relay[first][h].start()
        t_left[second][h].wait_recv()
        t_relay[2 + second][h].start()

    op[...] = turned(otown[...], PAD)

    @pl.when(is_same)
    def _():
        for w in range(2):
            for h in range(2):
                turn(w, h)

    cut_kernel(1)
    pass_on(0, 0)
    cut_kernel(2)
    cut_kernel(3)
    kb[:, pl.ds(PTS, ROWS - PTS), :] = jnp.zeros((8, ROWS - PTS, 2 * PAD), BF16)
    o_far[0].wait_recv()
    o_far[1].wait_recv()
    start(*o_relay[2])

    pass_on(1, 0)
    for h in range(2):
        o_sib[h].wait_recv()

    @pl.when(is_same)
    def _():
        for h in range(2):
            t_sib[0][h].wait_recv()
            run(0, h)

    arrive(0, 0, 0)
    pass_on(0, 1)

    @pl.when(is_cross)
    def _():
        for h in range(2):
            t_sib[0][h].wait_recv()
            run(0, h)

    pass_on(1, 1)
    arrive(1, 1, 0)
    start(t_far[0][0], t_far[1][0])

    for h in range(2):
        t_sib[1][h].wait_recv()
    run(1, 0)
    for i in (0, 1):
        for h in range(2):
            o_relay[i][h].wait_recv()
    t_relay[0][0].wait_recv()
    run(4, 0)
    t_relay[2][0].wait_recv()
    run(6, 0)
    arrive(0, 0, 1)
    t_relay[1][0].wait_recv()
    run(5, 0)
    t_relay[3][0].wait_recv()
    run(7, 0)
    arrive(1, 1, 1)
    start(t_far[0][1], t_far[1][1])
    run(1, 1)
    t_relay[0][1].wait_recv()
    run(4, 1)
    t_relay[2][1].wait_recv()
    run(6, 1)

    @pl.when(is_same)
    def _():
        for w in range(2):
            for h in range(2):
                t_sibz[w][h].wait_recv()
                run(2 + w, h)

    lax.fori_loop(1, 16, d_wait, 0)
    potential()

    t_far[0][0].wait_recv()
    t_relay[4][0].start()
    t_far[1][0].wait_recv()
    t_relay[5][0].start()
    t_relay[1][1].wait_recv()
    run(5, 1)
    t_relay[3][1].wait_recv()
    run(7, 1)
    for h in range(2):
        o_relay[2][h].wait_recv()
    t_relay[4][0].wait_recv()
    run(8, 0)
    t_relay[5][0].wait_recv()
    run(9, 0)
    t_far[0][1].wait_recv()
    t_relay[4][1].start()
    t_far[1][1].wait_recv()
    t_relay[5][1].start()
    t_relay[4][1].wait_recv()
    run(8, 1)
    t_relay[5][1].wait_recv()
    run(9, 1)

    row = lax.broadcasted_iota(jnp.int32, (8, 128), 0)
    tile = jnp.zeros((8, 128), F32)
    for side in range(4):
        tile = jnp.where(row == (zl * 2 + side) % 4, -0.5 * jnp.sum(exch[side]), tile)
    for w in range(2):
        tile = jnp.where(row == 4 + zl * 2 + w,
                         0.5 * jnp.sum(dens[pl.ds(w, 1), pl.ds(0, PTS)] * pot[pl.ds(w, 1), pl.ds(0, PTS)]), tile)
    ebuf[plane] = tile

    def e_flow(r):
        return pltpu.make_async_remote_copy(
            src_ref=ebuf.at[plane], dst_ref=ebuf.at[plane], send_sem=e_send.at[r], recv_sem=e_recv.at[r],
            device_id=plane_dev(r), device_id_type=MESH)

    def e_start(r, carry):
        e_flow(r).start()
        return carry

    def e_wait(r, carry):
        e_flow(r).wait()
        return carry

    lax.fori_loop(1, 32, e_start, 0)

    for pairs in (c_own, c_mate, c_far, c_matefar, t_z, t_right, t_left, t_sib, t_far, t_relay, o_relay):
        for pair in pairs:
            for cp in pair:
                cp.wait_send()
    for cp in c_z + o_first + o_far:
        cp.wait_send()

    @pl.when(is_cross)
    def _():
        for cp in o_xx + t_xx[0] + t_xx[1]:
            cp.wait_send()

    @pl.when(is_same)
    def _():
        for cp in t_sibz[0] + t_sibz[1]:
            cp.wait_send()

    lax.fori_loop(1, 32, e_wait, 0)
    sum_out[...] = ebuf[...].sum(axis=0)


def finish(pot, total, pot_out, cou_out, exc_out):
    zl = lax.axis_index("wlk") // 4
    pot_out[...] = pot[...]
    row = lax.broadcasted_iota(jnp.int32, (8, 128), 0)
    for w in range(2):
        exc_out[w] = jnp.sum(jnp.where(row == zl * 2 + w, total[...], 0.0)) * (1.0 / 128)
        cou_out[w] = jnp.sum(jnp.where(row == 4 + zl * 2 + w, total[...], 0.0)) * (1.0 / 128)


def local(green_half, collocation, occupied, kernel):
    any_space = pl.BlockSpec(memory_space=pl.ANY)
    vmem = pltpu.VMEM
    in_vmem, in_smem = pl.BlockSpec(memory_space=vmem), pl.BlockSpec(memory_space=pltpu.SMEM)
    pot, total = pl.pallas_call(
        body,
        out_shape=(jax.ShapeDtypeStruct((2, PTS), F32), jax.ShapeDtypeStruct((8, 128), F32)),
        in_specs=[any_space] * 4,
        out_specs=(in_vmem, in_vmem),
        scratch_shapes=[
            vmem((DEEP, PTS), BF16),
            vmem((ELEC, PTS), BF16),
            vmem((2 * ELEC, 8 * DEEP), BF16),
            vmem((GROUPS, 2 * ELEC, 384), BF16),
            vmem((2, KCH, 16 * PTS), BF16),
            vmem((8, ROWS, 2 * PAD), BF16),
            vmem((GROUPS, DEEP_PAD, PAD), BF16),
            vmem((2 * ELEC, PAD), F32),
            vmem((2, ELEC, PAD), BF16),
            vmem((10, ELEC, 2 * PAD), BF16),
            vmem((4, PAD, 512), BF16),
            vmem((PAD, 512), BF16),
            vmem((ELEC, PAD), BF16),
            vmem((4, ELEC, 2 * PAD), BF16),
            vmem((512, PAD), F32),
            vmem((2, PAD), F32),
            vmem((16, 2, PAD), F32),
            vmem((32, 8, 128), F32),
            vmem((4, 8, 256), F32),
            vmem((2, ROWS), F32),
            pltpu.SemaphoreType.DMA((8,)),
            pltpu.SemaphoreType.DMA((FLOWS,)),
            pltpu.SemaphoreType.DMA((FLOWS,)),
            pltpu.SemaphoreType.DMA((16,)),
            pltpu.SemaphoreType.DMA((16,)),
            pltpu.SemaphoreType.DMA((32,)),
            pltpu.SemaphoreType.DMA((32,)),
        ],
        compiler_params=pltpu.CompilerParams(
            collective_id=0, has_side_effects=True, vmem_limit_bytes=67_000_000),
    )(green_half, collocation, occupied.T, kernel)
    return pl.pallas_call(
        finish,
        out_shape=(jax.ShapeDtypeStruct((2, PTS), F32), jax.ShapeDtypeStruct((2,), F32), jax.ShapeDtypeStruct((2,), F32)),
        in_specs=[in_vmem, in_vmem],
        out_specs=(in_vmem, in_smem, in_smem),
    )(pot, total)


def solution(mesh):
    placed = (P("wlk", None, None), P("wlk", "pts"), P("pts", None), P("pts", None))
    return jax.shard_map(
        local,
        mesh=mesh,
        in_specs=placed,
        out_specs=(P("wlk", "pts"), P("wlk"), P("wlk")),
        check_vma=False,
    )
```

time: 261 us -> 103 us (0.39)
  Pallas kernels: 0 us -> 102 us
  waiting for transfers between devices: 88.6 us -> 0 us
  matrix products: 58.9 us -> 0 us
  starting transfers between devices: 40 us -> 0 us
  blocking collectives: 27 us -> 0 us
  local copies, waits for them, and re-layouts: 15.9 us -> 0 us
  other arithmetic: 15.8 us -> 0 us
  between operations: 14.2 us -> 0.8 us
    pallas_call x0 -> x2, Pallas kernels: none -> 102 us  [the longest x1 101 us: local(): pl.pallas_call(body, out_shape=(jax.ShapeDtypeStruct((2, PTS), F32), jax....]
    ppermute x16 -> x0, waiting for transfers between devices: 82.1 us -> none  [passed_along(): return lax.ppermute(block, axis, route)]
    dot_general x19 -> x0, matrix products: 58.9 us -> none  [the longest x9 28.3 us: block_terms(): jnp.einsum('awi,bi->wab', theta, occ_far, preferred_element_type=jnp.floa...]
    all_to_all x1 -> x0, blocking collectives: 27 us -> none  [from_everyone(): return lax.all_to_all(copies, axis, split_axis=0, concat_axis=0, tiled=True)]
    all_to_all x1 -> x0, starting transfers between devices: 20.4 us -> none  [from_everyone(): return lax.all_to_all(copies, axis, split_axis=0, concat_axis=0, tiled=True)]
    ppermute x16 -> x0, starting transfers between devices: 19.6 us -> none  [passed_along(): return lax.ppermute(block, axis, route)]
    convert_element_type x2 -> x0, other arithmetic: 10.8 us -> none  [the longest x1 10.8 us: block_terms(): lax.dynamic_slice_in_dim(kernel, start, occ_far.shape[0], 1)]
    unnamed x57 -> x0, local copies, waits for them, and re-layouts: 7.79 us -> none
  transfers between devices with their start and end apart: 18 -> 0, of which waited for: 11 -> 0; matrix products, arithmetic and copies ran while one was open for 33% -> 0% of each run, Pallas kernels for 0% -> 0%
where the time goes in v1:
time: 103 us
  Pallas kernels  102 us (99%)
    pallas_call x1, Pallas kernels, local(): pl.pallas_call(body, out_shape=(jax.ShapeDtypeStruct((2, PTS), F32), jax....  101 us

profile of v1, /device:TPU:1, one launch (start us, length us, event | category | flops | bytes accessed | tf_op | source)
XLA Modules:
  0.0 102.7 jit_solution(5683579901072112817)
XLA Ops:
  0.6 100.5 %shard_map.67 = (f32[2,600]{1,0:T(2,128)}, f32[8,128]{1,0:T(8,128)}) custom-call(bf16[2,400,2400]{2,1,0:T(8,128)(2,1)} %green.1, bf16[300,600]{1,0:T(8,128)(2,1)} %colloc.1, bf16[400,600]{1,0:T(8,128)(2,1)} %bitcast.1, bf16[600,9600]{1,0:T(8,128)(2,1)} %kmat.1), custom_call_target="tpu_custom_call" | custom-call | tf_op jit(solution)/shard_map/pallas_call | solution.py:528
  101.2 1.3 %shard_map.68 = (f32[2,600]{1,0:T(2,128)}, f32[2]{0:T(128)}, f32[2]{0:T(128)}) custom-call(f32[2,600]{1,0:T(2,128)} %get-tuple-element.5.pot, f32[8,128]{1,0:T(8,128)} %get-tuple-element.6.total), custom_call_target="tpu_custom_call" | custom-call | tf_op jit(solution)/shard_map/pallas_call | solution.py:565
